TPU v7x, 32 devices: a whole 2x2x4 slice. The times are simulated.
32 devices in a mesh: blk: 2 (over x), tp: 4 (over z), qg: 4 (over y, core).
Axes of the slice: x: 2, y: 2, z: 4, core: 2. Of those that a mesh axis runs over, the one named last changes fastest.
Arguments:
- hidden_states: bfloat16 [1536, 4096], P(('blk', 'tp'), 'qg'), may hold values from -8 to 8
- query_states: bfloat16 [256, 4096], P('tp', 'qg'), may hold values from -8 to 8
- w_query: bfloat16 [4096, 4096], P('qg', 'tp'), may hold values from -0.25 to 0.25
- w_key: bfloat16 [4096, 1024], P('qg', 'tp'), may hold values from -0.09375 to 0.09375
- w_value: bfloat16 [4096, 1024], P('qg', 'tp'), may hold values from -0.09375 to 0.09375
- slot_order: int32 [4], replicated, may hold values from 0 to 3, each once
Outputs:
- attention: bfloat16 [1536, 4096], P(('blk', 'qg'), 'tp')
- decoded: bfloat16 [256, 4096], P('qg', 'tp')
Inputs may be any that keep to these rules, and one draw needn't show every extreme that they name: slot_order holds every number of 0 to 3 once.
All inputs are finite; a program needn't handle non-finite values.
Results may differ from a plain program's by a relative error of at most 0.00775.
The roundings to bfloat16 on the way count: a program that leaves them out, or rounds other values in their place, can miss the bound.
Values may be sent and summed in bfloat16 or wider, within the bound.
A program may use at most 128 MiB of HBM per device.

v0:
```python
import math

import jax
import jax.numpy as jnp
from jax import lax
from jax.sharding import PartitionSpec as P

HEAD_DIM = 128


rope_base = 500000.0
floor_value = -1e30


def slot_positions(slot_order, row_ids, span_len):
    slot_ids = jnp.arange(slot_order.shape[0], dtype=jnp.int32)
    picked = jnp.sum(
        jnp.where((row_ids // span_len)[:, None] == slot_ids[None, :], slot_order[None, :], 0),
        axis=1,
    )
    return picked * span_len + row_ids % span_len


def rotate(value_heads, position):
    full_dim = value_heads.shape[-1]
    half_dim = full_dim // 2
    frequency = jnp.float32(rope_base) ** (
        jnp.arange(half_dim, dtype=jnp.float32) * jnp.float32(-2.0 / full_dim)
    )
    angles = position[:, None] * frequency[None, :]
    cosine = jnp.cos(angles)[:, None, :]
    sine_table = jnp.sin(angles)[:, None, :]
    front_half = value_heads[..., :half_dim]
    back_half = value_heads[..., half_dim:]
    return jnp.concatenate(
        [
            front_half * cosine - back_half * sine_table,
            back_half * cosine + front_half * sine_table,
        ],
        axis=-1,
    )


def heads_first(queries, kv_heads, sharing):
    row_count = queries.shape[0]
    shaped = queries.reshape(row_count, kv_heads, sharing, queries.shape[-1])
    return jnp.transpose(shaped, (1, 0, 2, 3)).reshape(
        kv_heads, row_count * sharing, queries.shape[-1]
    )


def empty_state(kv_heads, row_count, head_dim):
    return (
        jnp.full((kv_heads, row_count), floor_value, jnp.float32),
        jnp.zeros((kv_heads, row_count), jnp.float32),
        jnp.zeros((kv_heads, row_count, head_dim), jnp.float32),
    )


def block_update(carried, queries, key_heads, value_heads, allowed):
    running_max, normalizer, weighted = carried
    scaling = 1.0 / math.sqrt(queries.shape[-1])
    scores = (
        jnp.einsum("gqd,kgd->gqk", queries, key_heads, preferred_element_type=jnp.float32) * scaling
    )
    if allowed is not None:
        scores = jnp.where(allowed[None, :, :], scores, -jnp.inf)
    new_max = jnp.maximum(running_max, jnp.max(scores, axis=-1))
    weights = jnp.exp(scores - new_max[..., None])
    shrink = jnp.exp(running_max - new_max)
    normalizer = normalizer * shrink + jnp.sum(weights, axis=-1)
    product = jnp.einsum(
        "gqk,kgd->gqd",
        weights.astype(jnp.bfloat16),
        value_heads,
        preferred_element_type=jnp.float32,
    )
    return (new_max, normalizer, weighted * shrink[..., None] + product)


def key_step(row_count, shard_rows):
    chosen = shard_rows
    factor = 2
    while shard_rows * factor <= 1024 and shard_rows * factor <= row_count:
        if row_count % (shard_rows * factor) == 0:
            chosen = shard_rows * factor
        factor = factor + 1
    return chosen


def run_blocks(
    carried, pieces, first_row, queries, query_pos, slot_order, span_len, shard_rows, masked
):
    row_count = pieces.shape[0]
    block_len = key_step(row_count, shard_rows)
    kv_cols = pieces.shape[1] // 2
    kv_heads = queries.shape[0]
    head_dim = queries.shape[2]
    first_row = jnp.asarray(first_row)

    def one_block(turn_index, inner_state):
        offset = turn_index * block_len
        key_block = lax.dynamic_slice_in_dim(pieces, offset, block_len, 0)
        key_heads = key_block[:, :kv_cols].reshape(block_len, kv_heads, head_dim)
        value_heads = key_block[:, kv_cols:].reshape(block_len, kv_heads, head_dim)
        if not masked:
            return block_update(inner_state, queries, key_heads, value_heads, None)
        key_pos = slot_positions(
            slot_order, offset + jnp.arange(block_len, dtype=jnp.int32), span_len
        )
        allowed = key_pos[None, :] <= query_pos[:, None]
        return block_update(inner_state, queries, key_heads, value_heads, allowed)

    return lax.fori_loop(0, row_count // block_len, one_block, carried)


def finish(carried, row_count, sharing):
    running_max, normalizer, weighted = carried
    kv_heads = weighted.shape[0]
    head_dim = weighted.shape[2]
    result = (weighted / normalizer[..., None]).reshape(kv_heads, row_count, sharing, head_dim)
    return (
        jnp.transpose(result, (1, 0, 2, 3))
        .reshape(row_count, kv_heads * sharing * head_dim)
        .astype(jnp.bfloat16)
    )


def body(hidden_states, query_states, w_query, w_key, w_value, slot_order):
    block_rows, query_rows = (
        lax.all_gather(hidden_states, "tp", axis=0, tiled=True),
        lax.all_gather(query_states, "tp", axis=0, tiled=True),
    )
    qg_count = lax.axis_size("qg")
    member = lax.axis_index("qg")
    blk_index = lax.axis_index("blk")
    head_dim = HEAD_DIM
    heads_local = w_query.shape[1] // head_dim
    kv_heads = w_key.shape[1] // head_dim
    sharing = heads_local // kv_heads
    kv_cols = w_key.shape[1]
    group_rows = block_rows.shape[0]
    span_len = group_rows // 2
    own_rows = group_rows // qg_count
    own_queries = query_rows.shape[0] // qg_count
    columns = block_rows.shape[1]
    seq_len = group_rows * lax.axis_size("blk")
    stacked = jnp.concatenate(
        [
            block_rows.reshape(qg_count, own_rows, columns),
            query_rows.reshape(qg_count, own_queries, columns),
        ],
        axis=1,
    ).reshape(qg_count * (own_rows + own_queries), columns)
    query_sum = lax.psum_scatter(
        jnp.dot(stacked, w_query, preferred_element_type=jnp.float32),
        "qg",
        scatter_dimension=0,
        tiled=True,
    )
    partial_value = jnp.dot(
        block_rows, jnp.concatenate([w_key, w_value], axis=1), preferred_element_type=jnp.float32
    )
    kv_sum = lax.psum(partial_value, "qg")
    kv_start = blk_index * group_rows
    kv_rows = kv_sum.shape[0]
    key_pos = slot_positions(slot_order, kv_start + jnp.arange(kv_rows, dtype=jnp.int32), span_len)
    key_heads = rotate(
        kv_sum[:, :kv_cols].reshape(kv_rows, kv_heads, head_dim), key_pos.astype(jnp.float32)
    )
    kv_cache = jnp.concatenate(
        [
            key_heads.reshape(kv_rows, kv_cols).astype(jnp.bfloat16),
            kv_sum[:, kv_cols:].astype(jnp.bfloat16),
        ],
        axis=1,
    )
    query_start = blk_index * group_rows + member * own_rows
    query_pos = slot_positions(
        slot_order, query_start + jnp.arange(own_rows, dtype=jnp.int32), span_len
    )
    queries = rotate(
        query_sum[:own_rows].reshape(own_rows, heads_local, head_dim), query_pos.astype(jnp.float32)
    ).astype(jnp.bfloat16)
    queries = heads_first(queries, kv_heads, sharing)
    repeated = jnp.repeat(query_pos, sharing)
    fresh_pos = jnp.full((own_queries,), seq_len, jnp.float32)
    decode_query = rotate(
        query_sum[own_rows:].reshape(own_queries, heads_local, head_dim), fresh_pos
    ).astype(jnp.bfloat16)
    asked = heads_first(decode_query, kv_heads, sharing)
    starting = (
        empty_state(kv_heads, own_rows * sharing, head_dim),
        empty_state(kv_heads, own_queries * sharing, head_dim),
    )
    pieces = lax.all_gather(kv_cache, "blk", axis=0, tiled=True)
    first_row = jnp.int32(0)
    prefill_state = run_blocks(
        starting[0], pieces, first_row, queries, repeated, slot_order, span_len, kv_rows, True
    )
    decode_state = run_blocks(
        starting[1], pieces, first_row, asked, None, slot_order, span_len, kv_rows, False
    )
    carried, decode_state = (prefill_state, decode_state)
    decoded = finish(decode_state, own_queries, sharing)
    attention = finish(carried, own_rows, sharing)
    return (attention, decoded)


def solution(mesh):
    return jax.shard_map(
        body,
        mesh=mesh,
        in_specs=(
            P(("blk", "tp"), "qg"),
            P("tp", "qg"),
            P("qg", "tp"),
            P("qg", "tp"),
            P("qg", "tp"),
            P(),
        ),
        out_specs=(P(("blk", "qg"), "tp"), P("qg", "tp")),
        check_vma=False,
    )
```

profile of v0, /device:TPU:5, one launch (start us, length us, event | category | flops | bytes accessed | tf_op | source)
XLA Modules:
  0.0 198.4 jit_solution(10457108261832202985)
XLA Ops:
  7.2 0.0 all-gather.3.cloned.1.call-start
  7.2 0.7 all-gather.3.cloned.1.call-update
  7.9 0.0 all-reduce.2.cloned.1.call-start
  8.0 39.0 %all-gather.3.cloned.1.call-done = bf16[768,1024]{1,0:T(8,128)(2,1)} async-done(((bf16[192,1024]{1,0:T(8,128)(2,1)}), bf16[768,1024]{1,0:T(8,128)(2,1)}) %all-gather.3.cloned.1.call-update) | async-done | bytes 1572880 | tf_op jit(solution)/shard_map/all_gather | solution.py:131
  46.9 3.9 %convolution_bitcast_fusion = f32[768,512]{0,1:T(8,128)} fusion(bf16[768,1024]{1,0:T(8,128)(2,1)} %all-gather.3.cloned.1.call-done, bf16[1024,256]{1,0:T(8,128)(2,1)} %param.14, bf16[1024,256]{1,0:T(8,128)(2,1)} %param.13), kind=kOutput, calls=%fused_computation.47 | convolution fusion | flops 807403520 | bytes 4194304 | tf_op jit(solution)/shard_map/dot_general | solution.py:161
  50.9 0.0 all-reduce.2.cloned.1.call-update
  50.9 0.0 reduce-scatter.2.cloned.1.call-start
  51.0 13.1 %all_gather.11 = bf16[256,1024]{1,0:T(8,128)(2,1)S(1)} all-gather(bf16[64,1024]{1,0:T(8,128)(2,1)S(1)} %copy-done.3), channel_id=1, replica_groups=mesh['blk'=2,'tp'=4,'qg'=4] {'tp'}, dimensions={0}, use_global_device_ids=true | all-gather | bytes 655360 | tf_op jit(solution)/shard_map/all_gather | solution.py:132
  64.1 1.7 pad_maximum_fusion
  65.8 4.3 %fusion.46 = f32[1024,1024]{1,0:T(8,128)} fusion(bf16[1024,1024]{1,0:T(8,128)(2,1)S(1)} %bitcast.106, bf16[1024,1024]{1,0:T(8,128)(2,1)S(1)} %copy-done), kind=kOutput, calls=%fused_computation.100 | convolution fusion | flops 2147483648 | bytes 8388608 | tf_op jit(solution)/shard_map/dot_general | solution.py:156
  70.1 0.2 all-gather.5.cloned.1.call-start
  70.4 0.3 copy-done.4
  70.7 0.1 select_reduce_fusion.2
  70.8 0.1 select_reduce_fusion.1
  70.9 0.8 multiply_cosine_fusion
  71.7 21.0 %all-reduce.2.cloned.1.call-done = f32[768,512]{0,1:T(8,128)} async-done(((f32[768,512]{0,1:T(8,128)}), f32[768,512]{0,1:T(8,128)}) %all-reduce.2.cloned.1.call-update) | async-done | bytes 1572880 | tf_op jit(solution)/shard_map/psum | solution.py:164
  92.7 1.2 slice.104
  93.9 0.1 slice-done
  94.1 0.1 subtract_convert_fusion.1
  94.2 0.9 pad_maximum_fusion.1
  95.2 0.4 multiply_cosine_fusion.1
  95.7 44.1 %reduce-scatter.2.cloned.1.call-done = f32[256,1024]{1,0:T(8,128)} async-done(((f32[1024,1024]{1,0:T(8,128)}), f32[256,1024]{1,0:T(8,128)}) %reduce-scatter.2.cloned.1.call-update) | async-done | bytes 1048592 | tf_op jit(solution)/shard_map/reduce_scatter | solution.py:155
  139.8 1.2 slice_bitcast_fusion
  141.0 0.1 copy.50
  141.1 0.4 subtract_convert_fusion
  141.5 0.5 pad_maximum_fusion.3
  142.1 0.1 copy.48
  142.2 1.0 slice_bitcast_fusion.1
  143.3 0.1 subtract_convert_fusion.2
  143.4 0.2 pad_maximum_fusion.4
  143.7 25.7 %all-gather.5.cloned.1.call-done = bf16[1536,512]{0,1:T(8,128)(2,1)} async-done(((bf16[768,512]{0,1:T(8,128)(2,1)}), bf16[1536,512]{0,1:T(8,128)(2,1)}) %all-gather.5.cloned.1.call-update) | async-done | bytes 1572880 | tf_op jit(solution)/shard_map/all_gather | solution.py:196
  169.3 4.8 %while.39 = (s32[]{:T(128)}, f32[2,256]{1,0:T(2,128)S(1)}, f32[2,256]{1,0:T(2,128)S(1)}, f32[2,256,128]{2,1,0:T(8,128)S(1)}, bf16[1536,512]{0,1:T(8,128)(2,1)}, ...) while((s32[]{:T(128)}, f32[2,256]{1,0:T(2,128)S(1)}, ...), condition=%wide.region_12.13_spmd.clone, body=%wide.region_9.12_spmd.clone.sunk | while | flops 203885056 | bytes 7766211 | solution.py:114
  169.3 1.2 fusion.90
  170.5 0.4 bitcast_reduce_fusion.2
  170.9 0.2 fusion.92
  171.2 0.5 convolution_add_fusion.2
  171.7 1.2 fusion.90
  172.9 0.4 bitcast_reduce_fusion.2
  173.4 0.2 fusion.92
  173.6 0.5 convolution_add_fusion.2
  174.1 0.1 divide_convert_fusion.1
  174.3 0.7 convert_element_type.74
  175.1 14.2 %while.38 = (s32[]{:T(128)}, f32[2,768]{1,0:T(2,128)S(1)}, f32[2,768]{1,0:T(2,128)S(1)}, f32[2,768,128]{2,1,0:T(8,128)}, s32[4]{0:T(128)S(1)}, /*index=5*/bf16[1...) while((s32[]{:T(128)}, f32[2,768]{1,0:T(2,128)S(1)}, ...), condition=%wide.region_8.9_spmd.clone, body=%wide.region_4.8_spmd.clone.sunk | while | flops 618165504 | bytes 27261984 | solution.py:114
  175.1 0.1 select_reduce_fusion.4
  175.2 0.1 broadcast_in_dim.206
  175.3 0.1 le.52
  175.4 0.4 broadcast_compare_fusion.2
  175.8 1.2 fusion.80
  177.0 1.2 fusion.81
  178.2 1.1 fusion.83
  179.3 1.9 fusion.85
  181.3 0.9 copy-done.2
  182.2 0.1 select_reduce_fusion.4
  182.3 0.1 broadcast_in_dim.206
  182.4 0.1 le.52
  182.5 0.4 broadcast_compare_fusion.2
  182.9 1.2 fusion.80
  184.1 1.2 fusion.81
  185.3 1.1 fusion.83
  186.4 1.9 fusion.85
  188.4 0.9 copy-done.2
  189.3 1.4 divide_convert_fusion
  190.7 0.1 copy.54
  190.8 1.0 convert_element_type.70
  (46 shorter events, 0.6 us)
Async XLA Ops:
  7.2 58.6 %copy-start = (bf16[1024,1024]{1,0:T(8,128)(2,1)S(1)}, bf16[1024,1024]{1,0:T(8,128)(2,1)}, u32[]{:S(2)}) copy-start(bf16[1024,1024]{1,0:T(8,128)(2,1)} %param.12) | copy-start | bytes 6291460
  7.2 39.8 %all-gather.3.cloned.1.call-start = ((), (), s32[]{:S(2)}) async-start(), calls=%async_computation.1 | async-start | bytes 1966080 | tf_op jit(solution)/shard_map/all_gather | solution.py:131
  7.9 43.0 %copy-start.3 = (bf16[64,1024]{1,0:T(8,128)(2,1)S(1)}, bf16[64,1024]{1,0:T(8,128)(2,1)}, u32[]{:S(2)}) copy-start(bf16[64,1024]{1,0:T(8,128)(2,1)} %param.11) | copy-start | bytes 393220
  7.9 84.8 %all-reduce.2.cloned.1.call-start = ((), (), s32[]{:S(2)}) async-start(), calls=%async_computation.2 | async-start | bytes 3145728 | tf_op jit(solution)/shard_map/psum | solution.py:164
  50.9 88.9 %reduce-scatter.2.cloned.1.call-start = ((), (), s32[]{:S(2)}) async-start(), calls=%async_computation.4 | async-start | bytes 5242880 | tf_op jit(solution)/shard_map/reduce_scatter | solution.py:155
  70.1 0.7 copy-start.4
  70.1 99.2 %all-gather.5.cloned.1.call-start = ((), (), s32[]{:S(2)}) async-start(), calls=%async_computation.3 | async-start | bytes 2359296 | tf_op jit(solution)/shard_map/all_gather | solution.py:196
  92.7 1.4 slice-start
  178.2 1.1 copy-start.1
  181.2 0.9 copy-start.2
  185.3 1.1 copy-start.1
  188.3 0.9 copy-start.2
Sparse Core Ops, SparseCore 0:
  9.6 37.3 all-gather.2
  51.0 41.6 all-reduce.1
  95.2 44.5 reduce-scatter.1
  141.2 28.1 all-gather.4
where the time goes:
time: 201 us; the launch traced here: 198 us
  waiting for transfers between devices  130 us (65%)
  matrix products  16.3 us (8%)
  between operations  14 us (7%)
  local copies, waits for them, and re-layouts  13.1 us (7%)
  blocking collectives  13.1 us (7%)
  other arithmetic  10.8 us (5%)
    reduce_scatter x1, waiting for transfers between devices, body(): lax.psum_scatter(jnp.dot(stacked, w_query, preferred_element_type=jnp.flo...  44.1 us
    all_gather x1, waiting for transfers between devices, body(): lax.all_gather(hidden_states, 'tp', axis=0, tiled=True)  39 us
    all_gather x1, waiting for transfers between devices, body(): pieces = lax.all_gather(kv_cache, 'blk', axis=0, tiled=True)  25.7 us
    psum x1, waiting for transfers between devices, body(): kv_sum = lax.psum(partial_value, 'qg')  21 us
    all_gather x1, blocking collectives, body(): lax.all_gather(query_states, 'tp', axis=0, tiled=True)  13.1 us
    dot_general x4, matrix products, block_update(): jnp.einsum('gqk,kgd->gqd', weights.astype(jnp.bfloat16), value_heads, pre...  4.86 us
    slice x4, local copies, waits for them, and re-layouts, one_block(): value_heads = key_block[:, kv_cols:].reshape(block_len, kv_heads, head_dim)  4.69 us
    dot_general x1, matrix products, body(): jnp.dot(stacked, w_query, preferred_element_type=jnp.float32)  4.3 us
  transfers between devices with their start and end apart: 4, of which 4 were waited for; matrix products, arithmetic and copies ran while one was open for 7% of the time, Pallas kernels for 0%

commit v1 on v0

v1 whole, which is shorter than its diff:
```python
import functools
import math

import jax
import jax.numpy as jnp
import numpy as np
from jax import lax
from jax.experimental import pallas as pl
from jax.experimental.pallas import tpu as pltpu
from jax.sharding import PartitionSpec as P

HEAD_DIM = 128
ROPE_BASE = 500000.0
FLOOR = -1e30
TILE = 256
MESH = pl.DeviceIdType.MESH


def swap_halves(v):
    return pltpu.roll(v, HEAD_DIM // 2, 1)


def kernel(
    dims,
    slot,
    freq,
    hid,
    dec,
    wq_in,
    wk_in,
    wv_in,
    att_out,
    dec_out,
    own,
    xbuf,
    wq,
    wkv,
    qpart,
    qrecv,
    kvpart,
    kvrecv,
    kvall,
    qfin,
    sbuf,
    lsem,
    osem,
    xs,
    xr,
    ws,
    wr,
    qs,
    qr,
    ks_sem,
    kr_sem,
    cs_sem,
    cr_sem,
):
    nb, nz, nq, span = dims
    b = lax.axis_index("blk")
    z = lax.axis_index("tp")
    q = lax.axis_index("qg")
    c = lax.rem(q, 2)
    y = q // 2
    sib = (b, z, q + 1 - 2 * c)
    yp = (b, z, lax.rem(q + 2, nq))
    rows = hid.shape[0]
    drows = dec.shape[0]
    all_rows = rows + drows
    kvc = wk_in.shape[1]
    nt = wq_in.shape[1] // TILE
    heads = wq_in.shape[1] // HEAD_DIM
    kvh = kvc // HEAD_DIM
    sharing = heads // kvh
    group = rows * nz
    seq = group * nb
    kz = z // 2
    is_handler = lax.rem(z, 2) == c

    def local_x(dst):
        return (
            pltpu.make_async_copy(hid, dst.at[pl.ds(0, rows)], lsem.at[0]),
            pltpu.make_async_copy(dec, dst.at[pl.ds(rows, drows)], lsem.at[1]),
        )

    @pl.when(is_handler)
    def _():
        for cp in local_x(xbuf.at[kz, c]):
            cp.start()

    @pl.when(jnp.logical_not(is_handler))
    def _():
        for cp in local_x(own):
            cp.start()

    wlocal = (
        pltpu.make_async_copy(wq_in, wq.at[c], lsem.at[2]),
        pltpu.make_async_copy(wk_in, wkv.at[c, :, pl.ds(0, kvc)], lsem.at[3]),
        pltpu.make_async_copy(wv_in, wkv.at[c, :, pl.ds(kvc, kvc)], lsem.at[4]),
    )
    for cp in wlocal:
        cp.start()

    bar = pltpu.get_barrier_semaphore()

    def greet(dev):
        pl.semaphore_signal(bar, inc=1, device_id=dev, device_id_type=MESH)

    greet(sib)
    greet(yp)
    for o in range(1, nb):
        ob = lax.rem(b + o, nb)
        greet((ob, z, q))
        greet((ob, z, q + 1 - 2 * c))

    @pl.when(z > 0)
    def _():
        greet((b, z - 1, q))

    @pl.when(z < nz - 1)
    def _():
        greet((b, z + 1, q))

    @pl.when(jnp.logical_or(z == 0, z == nz - 1))
    def _():
        pl.semaphore_wait(bar, 2 + 2 * (nb - 1) + 1)

    @pl.when(jnp.logical_and(z > 0, z < nz - 1))
    def _():
        pl.semaphore_wait(bar, 2 + 2 * (nb - 1) + 2)

    def remote(src, dst, ss, rs, dev):
        return pltpu.make_async_remote_copy(
            src_ref=src, dst_ref=dst, send_sem=ss, recv_sem=rs, device_id=dev, device_id_type=MESH
        )

    own_send = remote(own, xbuf.at[kz, c], osem, xr.at[kz, c], sib)

    @pl.when(is_handler)
    def _():
        for cp in local_x(xbuf.at[kz, c]):
            cp.wait()

    @pl.when(jnp.logical_not(is_handler))
    def _():
        for cp in local_x(own):
            cp.wait()
        own_send.start()

    wremote = (
        remote(wk_in, wkv.at[c, :, pl.ds(0, kvc)], ws.at[1], wr.at[1], sib),
        remote(wv_in, wkv.at[c, :, pl.ds(kvc, kvc)], ws.at[2], wr.at[2], sib),
        remote(wq_in, wq.at[c], ws.at[0], wr.at[0], sib),
    )

    def relay(k, h, act):
        s = 2 * k + c
        ref = xbuf.at[k, h]

        @pl.when(jnp.logical_and(z <= s, z > 0))
        def _():
            act(remote(ref, ref, xs.at[k, h, 0], xr.at[k, h], (b, z - 1, q)))

        @pl.when(jnp.logical_and(z >= s, z < nz - 1))
        def _():
            act(remote(ref, ref, xs.at[k, h, 1], xr.at[k, h], (b, z + 1, q)))

    def landed(k, h):
        ref = xbuf.at[k, h]
        remote(ref, ref, xs.at[k, h, 0], xr.at[k, h], sib).wait_recv()

    def arrive(k):
        @pl.when(2 * k + c != z)
        def _():
            landed(k, c)

        relay(k, c, lambda cp: cp.start())
        landed(k, 1 - c)
        relay(k, 1 - c, lambda cp: cp.start())

    def kv_exchange(k):
        return remote(kvpart.at[k], kvrecv.at[k], ks_sem.at[k], kr_sem.at[k], yp)

    def q_exchange(k, t):
        return remote(qpart.at[k, t], qrecv.at[t], qs.at[t], qr.at[t], yp)

    def project(k):
        for t in range(2 * kvc // TILE):
            cols = pl.ds(t * TILE, TILE)
            kvpart[k, :, cols] = jnp.dot(
                xbuf[k, 0, :rows], wkv[0, :, cols], preferred_element_type=jnp.float32
            ) + jnp.dot(xbuf[k, 1, :rows], wkv[1, :, cols], preferred_element_type=jnp.float32)
        kv_exchange(k).start()

        def one(t, carry):
            cols = pl.ds(pl.multiple_of(t * TILE, TILE), TILE)
            qpart[k, t] = jnp.dot(
                xbuf[k, 0], wq[0, :, cols], preferred_element_type=jnp.float32
            ) + jnp.dot(xbuf[k, 1], wq[1, :, cols], preferred_element_type=jnp.float32)

            @pl.when(k != y)
            def _():
                q_exchange(k, t).start()

            return carry

        lax.fori_loop(0, nt, one, 0)

    lane = lax.broadcasted_iota(jnp.int32, (1, HEAD_DIM), 1)
    sign = jnp.where(lane < HEAD_DIM // 2, -1.0, 1.0).astype(jnp.float32)

    def block_pos(s):
        start = b * group + s * rows
        return slot[start // span] * span + lax.rem(start, span)

    def tables(pos):
        angles = pos.astype(jnp.float32) * freq[...]
        return jnp.cos(angles), jnp.sin(angles) * sign

    def cache_sends(k):
        s = 2 * k + c
        ref = kvall.at[b, s]
        devs = []
        for o in range(1, nb):
            ob = lax.rem(b + o, nb)
            devs += [(ob, z, q), (ob, z, q + 1 - 2 * c)]
        devs.append(sib)
        return [
            remote(ref, ref, cs_sem.at[k, i], cr_sem.at[b, s], dev) for i, dev in enumerate(devs)
        ]

    def finish_kv(k):
        s = 2 * k + c
        kv_exchange(k).wait_recv()
        total = kvpart[k] + kvrecv[k]
        pos = block_pos(s) + lax.broadcasted_iota(jnp.int32, (rows, 1), 0)
        cosine, sine = tables(pos)
        for g in range(kvh):
            v = total[:, g * HEAD_DIM : (g + 1) * HEAD_DIM]
            kvall[b, s, :, g * HEAD_DIM : (g + 1) * HEAD_DIM] = (
                v * cosine + swap_halves(v) * sine
            ).astype(jnp.bfloat16)
        kvall[b, s, :, kvc:] = total[:, kvc:].astype(jnp.bfloat16)
        for cp in cache_sends(k):
            cp.start()

    first = kz
    second = 1 - kz
    near = jnp.abs(z - 2 * first - c)
    far = jnp.abs(z - 2 * second - c)
    tie = near == far

    @pl.when(is_handler)
    def _():
        relay(kz, c, lambda cp: cp.start())

    for cp in wremote:
        cp.start()

    @pl.when(jnp.logical_not(is_handler))
    def _():
        landed(first, c)
        relay(first, c, lambda cp: cp.start())

    landed(first, 1 - c)
    relay(first, 1 - c, lambda cp: cp.start())

    @pl.when(tie)
    def _():
        arrive(second)

    for cp in wlocal:
        cp.wait()
    other = (
        remote(wk_in, wkv.at[1 - c, :, pl.ds(0, kvc)], ws.at[1], wr.at[1], sib),
        remote(wv_in, wkv.at[1 - c, :, pl.ds(kvc, kvc)], ws.at[2], wr.at[2], sib),
        remote(wq_in, wq.at[1 - c], ws.at[0], wr.at[0], sib),
    )
    for cp in other:
        cp.wait_recv()
    project(first)

    @pl.when(jnp.logical_not(tie))
    def _():
        arrive(second)
        finish_kv(first)

    project(second)

    @pl.when(tie)
    def _():
        finish_kv(first)

    finish_kv(second)

    row_id = lax.broadcasted_iota(jnp.int32, (all_rows, 1), 0)
    qpos = jnp.where(row_id < rows, block_pos(q) + row_id, seq)
    cosine, sine = tables(qpos)
    for t in range(nt):
        q_exchange(y, t).wait_recv()
        total = qpart[y, t] + qrecv[t]
        for h in range(TILE // HEAD_DIM):
            v = total[:, h * HEAD_DIM : (h + 1) * HEAD_DIM]
            qfin[t * (TILE // HEAD_DIM) + h] = (v * cosine + swap_halves(v) * sine).astype(
                jnp.bfloat16
            )

    for o in range(nb):
        ob = lax.rem(b + o, nb)
        for s in range(nz):
            ref = kvall.at[ob, s]
            wait = remote(ref, ref, cs_sem.at[0, 0], cr_sem.at[ob, s], sib).wait_recv
            if o == 0:
                pl.when(c != s % 2)(wait)
            else:
                wait()

    factor = math.log2(math.e) / math.sqrt(HEAD_DIM)
    unroll = nb <= 4

    def head(h, carry):
        qh = qfin[h]
        g = h // sharing
        kcols = pl.ds(pl.multiple_of(g * HEAD_DIM, HEAD_DIM), HEAD_DIM)
        vcols = pl.ds(pl.multiple_of(kvc + g * HEAD_DIM, HEAD_DIM), HEAD_DIM)

        def scores(j, m):
            keys = kvall[j, :, :, kcols].reshape(group, HEAD_DIM)
            s = lax.dot_general(
                qh, keys, (((1,), (1,)), ((), ())), preferred_element_type=jnp.float32
            )
            col = lax.broadcasted_iota(jnp.int32, (1, group), 1)
            kpos = jnp.zeros((1, group), jnp.int32)
            for i in range(group // span):
                inside = jnp.logical_and(col >= i * span, col < (i + 1) * span)
                kpos = jnp.where(
                    inside, slot[j * (group // span) + i] * span + col - i * span, kpos
                )
            s = jnp.where(kpos <= qpos, s, FLOOR)
            sbuf[j] = s
            return jnp.maximum(m, jnp.max(s, axis=1, keepdims=True))

        m = lax.fori_loop(
            0, nb, scores, jnp.full((all_rows, 1), FLOOR, jnp.float32), unroll=unroll
        )

        def weigh(j, state):
            norm, acc = state
            p = jnp.exp2((sbuf[j] - m) * factor)
            values = kvall[j, :, :, vcols].reshape(group, HEAD_DIM)
            norm = norm + jnp.sum(p, axis=1, keepdims=True)
            acc = acc + jnp.dot(
                p.astype(jnp.bfloat16), values, preferred_element_type=jnp.float32
            )
            return norm, acc

        norm, acc = lax.fori_loop(
            0,
            nb,
            weigh,
            (jnp.zeros((all_rows, 1), jnp.float32), jnp.zeros((all_rows, HEAD_DIM), jnp.float32)),
            unroll=unroll,
        )
        res = (acc / norm).astype(jnp.bfloat16)
        ocols = pl.ds(pl.multiple_of(h * HEAD_DIM, HEAD_DIM), HEAD_DIM)
        att_out[:, ocols] = res[:rows]
        dec_out[:, ocols] = res[rows:]
        return carry

    lax.fori_loop(0, heads, head, 0)

    @pl.when(jnp.logical_not(is_handler))
    def _():
        own_send.wait_send()

    for cp in wremote:
        cp.wait_send()
    for k in range(2):
        for h in range(2):
            relay(k, h, lambda cp: cp.wait_send())
        kv_exchange(k).wait_send()
        for cp in cache_sends(k):
            cp.wait_send()
    for t in range(nt):
        q_exchange(1 - y, t).wait_send()


def body(nb, nz, nq, hidden_states, query_states, w_query, w_key, w_value, slot_order):
    rows, depth = hidden_states.shape
    drows = query_states.shape[0]
    all_rows = rows + drows
    kvc = w_key.shape[1]
    nt = w_query.shape[1] // TILE
    heads = w_query.shape[1] // HEAD_DIM
    group = rows * nz
    span = group * nb // slot_order.shape[0]
    assert nz == 4 and nq == 4 and group % span == 0 and span % rows == 0
    exponent = np.arange(HEAD_DIM // 2, dtype=np.float64) * (-2.0 / HEAD_DIM)
    freq = np.float32(ROPE_BASE**exponent)
    freq = jnp.asarray(np.concatenate([freq, freq])[None, :])
    bf, f32 = jnp.bfloat16, jnp.float32
    dma = pltpu.SemaphoreType.DMA
    vm = pl.BlockSpec(memory_space=pltpu.VMEM)
    anyspace = pl.BlockSpec(memory_space=pl.ANY)
    return pl.pallas_call(
        functools.partial(kernel, (nb, nz, nq, span)),
        out_shape=(
            jax.ShapeDtypeStruct((rows, w_query.shape[1]), bf),
            jax.ShapeDtypeStruct((drows, w_query.shape[1]), bf),
        ),
        in_specs=[pl.BlockSpec(memory_space=pltpu.SMEM), vm] + [anyspace] * 5,
        out_specs=(vm, vm),
        scratch_shapes=[
            pltpu.VMEM((all_rows, depth), bf),
            pltpu.VMEM((2, 2, all_rows, depth), bf),
            pltpu.VMEM((2, depth, w_query.shape[1]), bf),
            pltpu.VMEM((2, depth, 2 * kvc), bf),
            pltpu.VMEM((2, nt, all_rows, TILE), f32),
            pltpu.VMEM((nt, all_rows, TILE), f32),
            pltpu.VMEM((2, rows, 2 * kvc), f32),
            pltpu.VMEM((2, rows, 2 * kvc), f32),
            pltpu.VMEM((nb, nz, rows, 2 * kvc), bf),
            pltpu.VMEM((heads, all_rows, HEAD_DIM), bf),
            pltpu.VMEM((nb, all_rows, group), f32),
            dma((5,)),
            dma,
            dma((2, 2, 2)),
            dma((2, 2)),
            dma((3,)),
            dma((3,)),
            dma((nt,)),
            dma((nt,)),
            dma((2,)),
            dma((2,)),
            dma((2, 2 * nb)),
            dma((nb, nz)),
        ],
        compiler_params=pltpu.CompilerParams(
            collective_id=0, has_side_effects=True, vmem_limit_bytes=60 * 1024 * 1024
        ),
    )(slot_order, freq, hidden_states, query_states, w_query, w_key, w_value)


def solution(mesh):
    sizes = (mesh.shape["blk"], mesh.shape["tp"], mesh.shape["qg"])
    return jax.shard_map(
        functools.partial(body, *sizes),
        mesh=mesh,
        in_specs=(
            P(("blk", "tp"), "qg"),
            P("tp", "qg"),
            P("qg", "tp"),
            P("qg", "tp"),
            P("qg", "tp"),
            P(),
        ),
        out_specs=(P(("blk", "qg"), "tp"), P("qg", "tp")),
        check_vma=False,
    )
```

time: 201 us -> 82.5 us (0.41); the launches traced: 198 us -> 82.1 us
  waiting for transfers between devices: 130 us -> 0 us
  Pallas kernels: 0 us -> 78.1 us
  matrix products: 16.3 us -> 0 us
  between operations: 14 us -> 0.64 us
  blocking collectives: 13.1 us -> 0 us
  other arithmetic: 10.8 us -> 0 us
  local copies, waits for them, and re-layouts: 13.1 us -> 3.33 us
    pallas_call x0 -> x1, Pallas kernels: none -> 78.1 us  [body(): pl.pallas_call(functools.partial(kernel, (nb, nz, nq, span)), out_shape=(...]
    all_gather x2 -> x0, waiting for transfers between devices: 64.6 us -> none  [the longest x1 39 us: body(): lax.all_gather(hidden_states, 'tp', axis=0, tiled=True)]
    reduce_scatter x1 -> x0, waiting for transfers between devices: 44.1 us -> none  [body(): lax.psum_scatter(jnp.dot(stacked, w_query, preferred_element_type=jnp.flo...]
    psum x1 -> x0, waiting for transfers between devices: 21 us -> none  [body(): kv_sum = lax.psum(partial_value, 'qg')]
    dot_general x10 -> x0, matrix products: 16.3 us -> none  [the longest x4 4.86 us: block_update(): jnp.einsum('gqk,kgd->gqd', weights.astype(jnp.bfloat16), value_heads, pre...]
    all_gather x1 -> x0, blocking collectives: 13.1 us -> none  [body(): lax.all_gather(query_states, 'tp', axis=0, tiled=True)]
    slice x7 -> x0, local copies, waits for them, and re-layouts: 6.05 us -> none  [the longest x4 4.69 us: one_block(): value_heads = key_block[:, kv_cols:].reshape(block_len, kv_heads, head_dim)]
    concatenate x5 -> x0, other arithmetic: 3.37 us -> none  [the longest x1 1.68 us: body(): jnp.concatenate([block_rows.reshape(qg_count, own_rows, columns), query_r...]
  transfers between devices with their start and end apart: 4 -> 0, of which waited for: 4 -> 0; matrix products, arithmetic and copies ran while one was open for 7% -> 0% of each run, Pallas kernels for 0% -> 0%
where the time goes in v1:
time: 82.5 us; the launch traced here: 82.1 us
  Pallas kernels  78.1 us (95%)
  local copies, waits for them, and re-layouts  3.33 us (4%)
    pallas_call x1, Pallas kernels, body(): pl.pallas_call(functools.partial(kernel, (nb, nz, nq, span)), out_shape=(...  78.1 us
    unnamed x2, local copies, waits for them, and re-layouts  3.33 us

profile of v1, /device:TPU:5, one launch (start us, length us, event | category | flops | bytes accessed | tf_op | source)
XLA Modules:
  0.0 82.1 jit_solution(14316268230961751116)
XLA Ops:
  0.6 78.1 %shard_map.86 = (bf16[192,1024]{1,0:T(8,128)(2,1)}, bf16[64,1024]{1,0:T(8,128)(2,1)}) custom-call(s32[4]{0:T(128)} %slot.1, f32[1,128]{1,0:T(1,128)} %constant.2.clone.freq, bf16[192,1024]{1,0:T(8,128)(2,1)} %hid.1, bf16[64,1024]{1,0:T(8,128)(2,1)} %dec.1, bf16[1024,1024]{1,0:T(8,128)(2,1)} %wq_in.1, bf16[1024,256]{1,0:T(8,128)(2,1)} %wk_in.1, ...), custom_call_target="tpu_custom_call" | custom-call | tf_op jit(solution)/shard_map/pallas_call | solution.py:404
  78.8 1.8 %copy.11 = bf16[192,1024]{1,0:T(8,128)(2,1)} copy(bf16[192,1024]{1,0:T(8,128)(2,1)} %get-tuple-element.4) | data formatting | bytes 786432
  80.5 1.6 %copy.12 = bf16[64,1024]{1,0:T(8,128)(2,1)} copy(bf16[64,1024]{1,0:T(8,128)(2,1)} %get-tuple-element.5) | data formatting | bytes 262144

commit v2 on v1

--- a/solution.py
+++ b/solution.py
@@ -40,7 +40,6 @@
     kvpart,
     kvrecv,
     kvall,
-    qfin,
     sbuf,
     lsem,
     osem,
@@ -68,9 +67,8 @@
     all_rows = rows + drows
     kvc = wk_in.shape[1]
     nt = wq_in.shape[1] // TILE
-    heads = wq_in.shape[1] // HEAD_DIM
     kvh = kvc // HEAD_DIM
-    sharing = heads // kvh
+    sharing = wq_in.shape[1] // kvc
     group = rows * nz
     seq = group * nb
     kz = z // 2
@@ -295,15 +293,6 @@
     row_id = lax.broadcasted_iota(jnp.int32, (all_rows, 1), 0)
     qpos = jnp.where(row_id < rows, block_pos(q) + row_id, seq)
     cosine, sine = tables(qpos)
-    for t in range(nt):
-        q_exchange(y, t).wait_recv()
-        total = qpart[y, t] + qrecv[t]
-        for h in range(TILE // HEAD_DIM):
-            v = total[:, h * HEAD_DIM : (h + 1) * HEAD_DIM]
-            qfin[t * (TILE // HEAD_DIM) + h] = (v * cosine + swap_halves(v) * sine).astype(
-                jnp.bfloat16
-            )
-
     for o in range(nb):
         ob = lax.rem(b + o, nb)
         for s in range(nz):
@@ -317,8 +306,7 @@
     factor = math.log2(math.e) / math.sqrt(HEAD_DIM)
     unroll = nb <= 4
 
-    def head(h, carry):
-        qh = qfin[h]
+    def head(h, qh, sbuf):
         g = h // sharing
         kcols = pl.ds(pl.multiple_of(g * HEAD_DIM, HEAD_DIM), HEAD_DIM)
         vcols = pl.ds(pl.multiple_of(kvc + g * HEAD_DIM, HEAD_DIM), HEAD_DIM)
@@ -364,9 +352,21 @@
         ocols = pl.ds(pl.multiple_of(h * HEAD_DIM, HEAD_DIM), HEAD_DIM)
         att_out[:, ocols] = res[:rows]
         dec_out[:, ocols] = res[rows:]
+
+    per = TILE // HEAD_DIM
+
+    def tile_heads(t, carry):
+        q_exchange(y, t).wait_recv()
+        total = qpart[y, t] + qrecv[t]
+        ready = []
+        for i in range(per):
+            v = total[:, i * HEAD_DIM : (i + 1) * HEAD_DIM]
+            ready.append((v * cosine + swap_halves(v) * sine).astype(jnp.bfloat16))
+        for i in range(per):
+            head(t * per + i, ready[i], sbuf.at[i] if nb <= 4 else sbuf.at[0])
         return carry
 
-    lax.fori_loop(0, heads, head, 0)
+    lax.fori_loop(0, nt, tile_heads, 0)
 
     @pl.when(jnp.logical_not(is_handler))
     def _():
@@ -390,7 +390,6 @@
     all_rows = rows + drows
     kvc = w_key.shape[1]
     nt = w_query.shape[1] // TILE
-    heads = w_query.shape[1] // HEAD_DIM
     group = rows * nz
     span = group * nb // slot_order.shape[0]
     assert nz == 4 and nq == 4 and group % span == 0 and span % rows == 0
@@ -419,8 +418,7 @@
             pltpu.VMEM((2, rows, 2 * kvc), f32),
             pltpu.VMEM((2, rows, 2 * kvc), f32),
             pltpu.VMEM((nb, nz, rows, 2 * kvc), bf),
-            pltpu.VMEM((heads, all_rows, HEAD_DIM), bf),
-            pltpu.VMEM((nb, all_rows, group), f32),
+            pltpu.VMEM((2 if nb <= 4 else 1, nb, all_rows, group), f32),
             dma((5,)),
             dma,
             dma((2, 2, 2)),

time: 82.5 us -> 76.5 us (0.927)
  Pallas kernels: 78.1 us -> 72.2 us
    pallas_call x1, Pallas kernels: 78.1 us -> 72.2 us  [body(): pl.pallas_call(functools.partial(kernel, (nb, nz, nq, span)), out_shape=(...]
where the time goes in v2:
time: 76.5 us; the launch traced here: 76.1 us
  Pallas kernels  72.2 us (94%)
  local copies, waits for them, and re-layouts  3.33 us (4%)
    pallas_call x1, Pallas kernels, body(): pl.pallas_call(functools.partial(kernel, (nb, nz, nq, span)), out_shape=(...  72.2 us
    unnamed x2, local copies, waits for them, and re-layouts  3.33 us

profile of v2, /device:TPU:5, one launch (start us, length us, event | category | flops | bytes accessed | tf_op | source)
XLA Modules:
  0.0 76.1 jit_solution(3279268551312483266)
XLA Ops:
  0.6 72.2 %shard_map.86 = (bf16[192,1024]{1,0:T(8,128)(2,1)}, bf16[64,1024]{1,0:T(8,128)(2,1)}) custom-call(s32[4]{0:T(128)} %slot.1, f32[1,128]{1,0:T(1,128)} %constant.2.clone.freq, bf16[192,1024]{1,0:T(8,128)(2,1)} %hid.1, bf16[64,1024]{1,0:T(8,128)(2,1)} %dec.1, bf16[1024,1024]{1,0:T(8,128)(2,1)} %wq_in.1, bf16[1024,256]{1,0:T(8,128)(2,1)} %wk_in.1, ...), custom_call_target="tpu_custom_call" | custom-call | tf_op jit(solution)/shard_map/pallas_call | solution.py:403
  72.8 1.8 %copy.11 = bf16[192,1024]{1,0:T(8,128)(2,1)} copy(bf16[192,1024]{1,0:T(8,128)(2,1)} %get-tuple-element.4) | data formatting | bytes 786432
  74.6 1.6 %copy.12 = bf16[64,1024]{1,0:T(8,128)(2,1)} copy(bf16[64,1024]{1,0:T(8,128)(2,1)} %get-tuple-element.5) | data formatting | bytes 262144

commit v3 on v2

--- a/solution.py
+++ b/solution.py
@@ -53,6 +53,9 @@
     kr_sem,
     cs_sem,
     cr_sem,
+    dbuf,
+    ds_sem,
+    dr_sem,
 ):
     nb, nz, nq, span = dims
     b = lax.axis_index("blk")
@@ -63,7 +66,9 @@
     sib = (b, z, q + 1 - 2 * c)
     yp = (b, z, lax.rem(q + 2, nq))
     rows = hid.shape[0]
-    drows = dec.shape[0]
+    split = dbuf.shape[0]
+    drows = dec.shape[0] // split
+    part = lax.rem(b, split)
     all_rows = rows + drows
     kvc = wk_in.shape[1]
     nt = wq_in.shape[1] // TILE
@@ -77,7 +82,11 @@
     def local_x(dst):
         return (
             pltpu.make_async_copy(hid, dst.at[pl.ds(0, rows)], lsem.at[0]),
-            pltpu.make_async_copy(dec, dst.at[pl.ds(rows, drows)], lsem.at[1]),
+            pltpu.make_async_copy(
+                dec.at[pl.ds(pl.multiple_of(part * drows, drows), drows)],
+                dst.at[pl.ds(rows, drows)],
+                lsem.at[1],
+            ),
         )
 
     @pl.when(is_handler)
@@ -305,6 +314,10 @@
 
     factor = math.log2(math.e) / math.sqrt(HEAD_DIM)
     unroll = nb <= 4
+
+    def decode_exchange(t):
+        ref = dbuf.at[part, t]
+        return remote(ref, ref, ds_sem.at[t], dr_sem.at[t], (b + 1 - 2 * part, z, q))
 
     def head(h, qh, sbuf):
         g = h // sharing
@@ -351,7 +364,7 @@
         res = (acc / norm).astype(jnp.bfloat16)
         ocols = pl.ds(pl.multiple_of(h * HEAD_DIM, HEAD_DIM), HEAD_DIM)
         att_out[:, ocols] = res[:rows]
-        dec_out[:, ocols] = res[rows:]
+        return res[rows:]
 
     per = TILE // HEAD_DIM
 
@@ -363,10 +376,23 @@
             v = total[:, i * HEAD_DIM : (i + 1) * HEAD_DIM]
             ready.append((v * cosine + swap_halves(v) * sine).astype(jnp.bfloat16))
         for i in range(per):
-            head(t * per + i, ready[i], sbuf.at[i] if nb <= 4 else sbuf.at[0])
+            res = head(t * per + i, ready[i], sbuf.at[i] if nb <= 4 else sbuf.at[0])
+            dbuf[part, t, :, i * HEAD_DIM : (i + 1) * HEAD_DIM] = res
+        if split == 2:
+            decode_exchange(t).start()
         return carry
 
     lax.fori_loop(0, nt, tile_heads, 0)
+
+    for t in range(nt):
+        if split == 2:
+            decode_exchange(t).wait_recv()
+        for i in range(split):
+            dec_out[i * drows : (i + 1) * drows, t * TILE : (t + 1) * TILE] = dbuf[i, t]
+
+    if split == 2:
+        for t in range(nt):
+            decode_exchange(t).wait_send()
 
     @pl.when(jnp.logical_not(is_handler))
     def _():
@@ -386,7 +412,8 @@
 
 def body(nb, nz, nq, hidden_states, query_states, w_query, w_key, w_value, slot_order):
     rows, depth = hidden_states.shape
-    drows = query_states.shape[0]
+    split = 2 if nb % 2 == 0 else 1
+    drows = query_states.shape[0] // split
     all_rows = rows + drows
     kvc = w_key.shape[1]
     nt = w_query.shape[1] // TILE
@@ -404,7 +431,7 @@
         functools.partial(kernel, (nb, nz, nq, span)),
         out_shape=(
             jax.ShapeDtypeStruct((rows, w_query.shape[1]), bf),
-            jax.ShapeDtypeStruct((drows, w_query.shape[1]), bf),
+            jax.ShapeDtypeStruct((drows * split, w_query.shape[1]), bf),
         ),
         in_specs=[pl.BlockSpec(memory_space=pltpu.SMEM), vm] + [anyspace] * 5,
         out_specs=(vm, vm),
@@ -431,6 +458,9 @@
             dma((2,)),
             dma((2, 2 * nb)),
             dma((nb, nz)),
+            pltpu.VMEM((split, nt, drows, TILE), bf),
+            dma((nt,)),
+            dma((nt,)),
         ],
         compiler_params=pltpu.CompilerParams(
             collective_id=0, has_side_effects=True, vmem_limit_bytes=60 * 1024 * 1024

time: 76.5 us -> 72.5 us (0.948)
  Pallas kernels: 72.2 us -> 68.3 us
    pallas_call x1, Pallas kernels: 72.2 us -> 68.3 us  [body(): pl.pallas_call(functools.partial(kernel, (nb, nz, nq, span)), out_shape=(...]
where the time goes in v3:
time: 72.5 us; the launch traced here: 72.3 us
  Pallas kernels  68.3 us (94%)
  local copies, waits for them, and re-layouts  3.33 us (5%)
    pallas_call x1, Pallas kernels, body(): pl.pallas_call(functools.partial(kernel, (nb, nz, nq, span)), out_shape=(...  68.3 us
    unnamed x2, local copies, waits for them, and re-layouts  3.33 us

profile of v3, /device:TPU:5, one launch (start us, length us, event | category | flops | bytes accessed | tf_op | source)
XLA Modules:
  0.0 72.3 jit_solution(10376723272039002007)
XLA Ops:
  0.6 68.3 %shard_map.86 = (bf16[192,1024]{1,0:T(8,128)(2,1)}, bf16[64,1024]{1,0:T(8,128)(2,1)}) custom-call(s32[4]{0:T(128)} %slot.1, f32[1,128]{1,0:T(1,128)} %constant.2.clone.freq, bf16[192,1024]{1,0:T(8,128)(2,1)} %hid.1, bf16[64,1024]{1,0:T(8,128)(2,1)} %dec.1, bf16[1024,1024]{1,0:T(8,128)(2,1)} %wq_in.1, bf16[1024,256]{1,0:T(8,128)(2,1)} %wk_in.1, ...), custom_call_target="tpu_custom_call" | custom-call | tf_op jit(solution)/shard_map/pallas_call | solution.py:430
  69.0 1.8 %copy.11 = bf16[192,1024]{1,0:T(8,128)(2,1)} copy(bf16[192,1024]{1,0:T(8,128)(2,1)} %get-tuple-element.4) | data formatting | bytes 786432
  70.8 1.6 %copy.12 = bf16[64,1024]{1,0:T(8,128)(2,1)} copy(bf16[64,1024]{1,0:T(8,128)(2,1)} %get-tuple-element.5) | data formatting | bytes 262144

commit v4 on v3

--- a/solution.py
+++ b/solution.py
@@ -56,6 +56,10 @@
     dbuf,
     ds_sem,
     dr_sem,
+    vsend,
+    vrecv,
+    vs_sem,
+    vr_sem,
 ):
     nb, nz, nq, span = dims
     b = lax.axis_index("blk")
@@ -184,19 +188,26 @@
         landed(k, 1 - c)
         relay(k, 1 - c, lambda cp: cp.start())
 
-    def kv_exchange(k):
-        return remote(kvpart.at[k], kvrecv.at[k], ks_sem.at[k], kr_sem.at[k], yp)
+    def k_exchange(k):
+        return remote(kvpart.at[k, 0], kvrecv.at[k], ks_sem.at[k], kr_sem.at[k], yp)
+
+    def v_exchange(k):
+        return remote(vsend.at[k], vrecv.at[k], vs_sem.at[k], vr_sem.at[k], yp)
 
     def q_exchange(k, t):
         return remote(qpart.at[k, t], qrecv.at[t], qs.at[t], qr.at[t], yp)
 
     def project(k):
-        for t in range(2 * kvc // TILE):
-            cols = pl.ds(t * TILE, TILE)
-            kvpart[k, :, cols] = jnp.dot(
+        for t in range(2):
+            cols = pl.ds(t * kvc, kvc)
+            kvpart[k, t] = jnp.dot(
                 xbuf[k, 0, :rows], wkv[0, :, cols], preferred_element_type=jnp.float32
             ) + jnp.dot(xbuf[k, 1, :rows], wkv[1, :, cols], preferred_element_type=jnp.float32)
-        kv_exchange(k).start()
+            if t == 0:
+                k_exchange(k).start()
+            else:
+                vsend[k] = kvpart[k, 1].astype(jnp.bfloat16)
+                v_exchange(k).start()
 
         def one(t, carry):
             cols = pl.ds(pl.multiple_of(t * TILE, TILE), TILE)
@@ -237,16 +248,17 @@
 
     def finish_kv(k):
         s = 2 * k + c
-        kv_exchange(k).wait_recv()
-        total = kvpart[k] + kvrecv[k]
         pos = block_pos(s) + lax.broadcasted_iota(jnp.int32, (rows, 1), 0)
         cosine, sine = tables(pos)
+        k_exchange(k).wait_recv()
+        total = kvpart[k, 0] + kvrecv[k]
         for g in range(kvh):
             v = total[:, g * HEAD_DIM : (g + 1) * HEAD_DIM]
             kvall[b, s, :, g * HEAD_DIM : (g + 1) * HEAD_DIM] = (
                 v * cosine + swap_halves(v) * sine
             ).astype(jnp.bfloat16)
-        kvall[b, s, :, kvc:] = total[:, kvc:].astype(jnp.bfloat16)
+        v_exchange(k).wait_recv()
+        kvall[b, s, :, kvc:] = (kvpart[k, 1] + vrecv[k].astype(jnp.float32)).astype(jnp.bfloat16)
         for cp in cache_sends(k):
             cp.start()
 
@@ -268,12 +280,18 @@
         landed(first, c)
         relay(first, c, lambda cp: cp.start())
 
+    @pl.when(tie)
+    def _():
+        landed(second, c)
+        relay(second, c, lambda cp: cp.start())
+
     landed(first, 1 - c)
     relay(first, 1 - c, lambda cp: cp.start())
 
     @pl.when(tie)
     def _():
-        arrive(second)
+        landed(second, 1 - c)
+        relay(second, 1 - c, lambda cp: cp.start())
 
     for cp in wlocal:
         cp.wait()
@@ -403,7 +421,8 @@
     for k in range(2):
         for h in range(2):
             relay(k, h, lambda cp: cp.wait_send())
-        kv_exchange(k).wait_send()
+        k_exchange(k).wait_send()
+        v_exchange(k).wait_send()
         for cp in cache_sends(k):
             cp.wait_send()
     for t in range(nt):
@@ -442,8 +461,8 @@
             pltpu.VMEM((2, depth, 2 * kvc), bf),
             pltpu.VMEM((2, nt, all_rows, TILE), f32),
             pltpu.VMEM((nt, all_rows, TILE), f32),
-            pltpu.VMEM((2, rows, 2 * kvc), f32),
-            pltpu.VMEM((2, rows, 2 * kvc), f32),
+            pltpu.VMEM((2, 2, rows, kvc), f32),
+            pltpu.VMEM((2, rows, kvc), f32),
             pltpu.VMEM((nb, nz, rows, 2 * kvc), bf),
             pltpu.VMEM((2 if nb <= 4 else 1, nb, all_rows, group), f32),
             dma((5,)),
@@ -461,6 +480,10 @@
             pltpu.VMEM((split, nt, drows, TILE), bf),
             dma((nt,)),
             dma((nt,)),
+            pltpu.VMEM((2, rows, kvc), bf),
+            pltpu.VMEM((2, rows, kvc), bf),
+            dma((2,)),
+            dma((2,)),
         ],
         compiler_params=pltpu.CompilerParams(
             collective_id=0, has_side_effects=True, vmem_limit_bytes=60 * 1024 * 1024

time: 72.5 us -> 70.8 us (0.977)
  Pallas kernels: 68.3 us -> 66.6 us
    pallas_call x1, Pallas kernels: 68.3 us -> 66.6 us  [body(): pl.pallas_call(functools.partial(kernel, (nb, nz, nq, span)), out_shape=(...]
where the time goes in v4:
time: 70.8 us; the launch traced here: 70.6 us
  Pallas kernels  66.6 us (94%)
  local copies, waits for them, and re-layouts  3.33 us (5%)
    pallas_call x1, Pallas kernels, body(): pl.pallas_call(functools.partial(kernel, (nb, nz, nq, span)), out_shape=(...  66.6 us
    unnamed x2, local copies, waits for them, and re-layouts  3.33 us

profile of v4, /device:TPU:5, one launch (start us, length us, event | category | flops | bytes accessed | tf_op | source)
XLA Modules:
  0.0 70.6 jit_solution(9696192984955760026)
XLA Ops:
  0.6 66.6 %shard_map.86 = (bf16[192,1024]{1,0:T(8,128)(2,1)}, bf16[64,1024]{1,0:T(8,128)(2,1)}) custom-call(s32[4]{0:T(128)} %slot.1, f32[1,128]{1,0:T(1,128)} %constant.2.clone.freq, bf16[192,1024]{1,0:T(8,128)(2,1)} %hid.1, bf16[64,1024]{1,0:T(8,128)(2,1)} %dec.1, bf16[1024,1024]{1,0:T(8,128)(2,1)} %wq_in.1, bf16[1024,256]{1,0:T(8,128)(2,1)} %wk_in.1, ...), custom_call_target="tpu_custom_call" | custom-call | tf_op jit(solution)/shard_map/pallas_call | solution.py:449
  67.3 1.8 %copy.11 = bf16[192,1024]{1,0:T(8,128)(2,1)} copy(bf16[192,1024]{1,0:T(8,128)(2,1)} %get-tuple-element.4) | data formatting | bytes 786432
  69.0 1.6 %copy.12 = bf16[64,1024]{1,0:T(8,128)(2,1)} copy(bf16[64,1024]{1,0:T(8,128)(2,1)} %get-tuple-element.5) | data formatting | bytes 262144
